TPU v7x, 512 devices: a 8x2x16 block of a 8x8x16 slice. The times are simulated.
512 devices in a mesh: stack: 2 (over y), date: 8 (over x), line: 32 (over z, core).
Axes of the slice: x: 8, y: 2, z: 16, core: 2. Of those that a mesh axis runs over, the one named last changes fastest.
The devices are a block of a 8x8x16 slice.
Arguments:
- slc: float32 [8, 2, 512, 10240], P('date', None, 'stack', 'line'), parts along dimension 2, may hold values from -6 to 6
- band_start: int32 [8], replicated, may hold values from 0 to 5120, as said below
- band_stop: int32 [8], replicated, may hold values from 5120 to 10240, as said below
Outputs:
- interferogram: float32 [8, 2, 512, 2048], P('date', None, 'stack', 'line'), parts along dimension 2
There are 2 independent parts, one for each index of `stack`. A program takes and returns all parts, laid end to end along the dimension named above; an argument that names none is the same for every part. Nothing has to cross between parts.
Inputs may be any that keep to these rules, and one draw needn't show every extreme that they name: For every pair, band_stop - band_start lies between 5120 and 7680; at least one pair keeps exactly 7680 bins, and some pair keeps exactly 5120 bins ending at 10240. `band_stop`: see band_start.
All inputs are finite; a program needn't handle non-finite values.
Results may differ from a plain program's by a relative error of at most 0.0001.
Values sent between devices are 32-bit elements; how exact they have to be, the bound alone decides.
A program may use at most 64 MiB of HBM per device.

v0:
```python
import functools
import math

import jax
import jax.numpy as jnp
import numpy as np
from jax import lax
from jax.experimental import pallas as pl
from jax.experimental.pallas import tpu as pltpu
from jax.sharding import PartitionSpec as P

LOOKS = 5
CORES = 2
GROUP = 4
LANES = 128
MESH = pl.DeviceIdType.MESH


def split_table(table):
    high = table.astype(jnp.bfloat16)
    low = (table - high.astype(np.float32)).astype(jnp.bfloat16)
    return np.stack([high, low])


@functools.lru_cache(maxsize=None)
def tables(outer, inner):
    whole = outer * inner
    bins = 2 * LANES
    tail = inner - bins
    eye = np.eye(GROUP)
    turn = 2 * np.pi / outer * (np.outer(np.arange(outer), np.arange(outer)) % outer)
    cos, sin = np.cos(turn), np.sin(turn)
    blocks = np.array([[cos, sin], [-sin, cos]])
    first = np.einsum("pqkd,x->pkdqx", blocks, np.ones(GROUP)).reshape(2 * outer, -1)
    last = np.einsum("qdk,cx->dcqxk", np.array([cos, sin]), eye).reshape(outer * GROUP, -1)
    line, bin_ = np.arange(inner), np.arange(bins)
    turn = 2 * np.pi / inner * (np.outer(line, bin_) % inner)
    cos, sin = np.cos(turn), np.sin(turn)
    from_re = np.concatenate([cos, -sin], 1)
    from_im = np.concatenate([sin, cos], 1)
    ahead = np.concatenate([from_re[:bins], from_im[:bins], from_re[bins:], from_im[bins:]])
    looks = inner // LOOKS
    order = (np.arange(looks)[None] * LOOKS + np.arange(LOOKS)[:, None]).reshape(-1)
    cos_o, sin_o = cos[order].T, sin[order].T
    to_re = np.concatenate([cos_o, -sin_o], 0).reshape(2 * bins, LOOKS, 1, looks)
    to_im = np.concatenate([sin_o, cos_o], 0).reshape(2 * bins, LOOKS, 1, looks)
    back = np.concatenate([to_re, to_im], 2).reshape(2 * bins, 2 * inner)
    k1 = np.arange(outer)
    lanes = np.concatenate([line, line[bins:]])
    turn = 2 * np.pi / whole * np.outer(k1, lanes)
    ahead_turn = np.stack([np.cos(turn), -np.sin(turn)])
    turn = 2 * np.pi / whole * np.outer(k1, order)
    cos, sin = (f(turn).reshape(-1, LOOKS, 1, looks) for f in (np.cos, np.sin))
    back_turn = np.stack(
        [
            np.concatenate([cos, cos], 2).reshape(-1, 2 * inner),
            np.concatenate([-sin, sin], 2).reshape(-1, 2 * inner),
        ]
    )
    assert 2 * tail == LANES and 2 * looks == LANES
    as_f32 = lambda a: a.astype(np.float32)
    return (
        split_table(as_f32(first)),
        split_table(as_f32(ahead)),
        split_table(as_f32(back)),
        split_table(as_f32(last)),
        as_f32(ahead_turn),
        as_f32(back_turn),
    )


def parts_of(values):
    high = values.astype(jnp.bfloat16)
    return high, (values - high.astype(jnp.float32)).astype(jnp.bfloat16)


def dot(a, b):
    return jnp.dot(a, b, preferred_element_type=jnp.float32)


def left(table, values):
    high, low = parts_of(values)
    return dot(table[0], high) + dot(table[0], low) + dot(table[1], high)


def right(values, table):
    high, low = parts_of(values)
    return dot(high, table[0]) + dot(low, table[0]) + dot(high, table[1])


def half_turned(values, roll):
    pieces = [
        roll(values[:, i : i + LANES]) for i in range(0, values.shape[1], LANES)
    ]
    return jnp.concatenate(pieces, 1)


def lane_index(shape):
    return lax.broadcasted_iota(jnp.int32, shape, 1)


def low_half(shape):
    return lane_index(shape) % LANES < LANES // 2


def start_turn(ahead_turn, start, outer, inner):
    lanes = lane_index((1, 3 * LANES))
    line = jnp.where(lanes < inner, lanes, lanes - (LANES // 2))
    steps = (line * (start // outer)).astype(jnp.float32)
    steps = steps - inner * jnp.floor((steps + 0.5) * (1.0 / inner))
    angle = steps * (2.0 * math.pi / inner)
    cos, sin = jnp.cos(angle), -jnp.sin(angle)
    real, imag = ahead_turn[0], ahead_turn[1]
    return for_columns(real * cos - imag * sin), for_columns(real * sin + imag * cos)


def first_table(first, outer):
    column = lane_index((2 * outer, first.shape[2])) % GROUP
    pieces = []
    for piece in (first[0], first[1]):
        wide = piece.astype(jnp.float32)
        own = [jnp.where(column == c, wide, 0.0) for c in range(GROUP)]
        rows = [v[:outer] for v in own] + [v[outer:] for v in own]
        pieces.append(jnp.concatenate(rows, 0).astype(jnp.bfloat16))
    return pieces


def for_columns(table):
    return jnp.concatenate([table] * GROUP, 0)


def lines_of(first, tiles, turn, second, roll):
    block = jnp.concatenate(tiles, 1)
    mixed = left(first, block)
    rows = mixed.shape[0] // 2
    real, imag = mixed[:rows], mixed[rows:]
    turned_real = real * turn[0] - imag * turn[1]
    turned_imag = real * turn[1] + imag * turn[0]
    main = 2 * LANES
    tail_real, tail_imag = turned_real[:, main:], turned_imag[:, main:]
    low = low_half(tail_real.shape)
    if second:
        tail = jnp.where(low, roll(tail_real), tail_imag)
    else:
        tail = jnp.where(low, tail_real, roll(tail_imag))
    return jnp.concatenate([turned_real[:, :main], turned_imag[:, :main], tail], 1)


def keep_mask(start, stop, outer, rows):
    shape = (rows, 2 * LANES)
    k1 = lax.broadcasted_iota(jnp.int32, shape, 0) % outer
    k = k1 + outer * (lane_index(shape) + start // outer)
    return (k >= start) & (k < stop)


def back_lines(spectrum, mask, back, back_turn, roll):
    bins = mask.shape[1]
    kept = jnp.concatenate(
        [jnp.where(mask, spectrum[:, :bins], 0.0), jnp.where(mask, spectrum[:, bins:], 0.0)], 1
    )
    lines = right(kept, back)
    return lines * for_columns(back_turn[0]) + half_turned(lines, roll) * for_columns(back_turn[1])


def signal_of(lines, last, roll):
    turned = half_turned(lines, roll)
    turned = jnp.where(low_half(turned.shape), -turned, turned)
    return left(last, jnp.concatenate([lines, turned], 0))


def looked(ref, sec, scale, roll):
    same = cross = None
    for i in range(LOOKS):
        a, b = (v[:, i * LANES : (i + 1) * LANES] for v in (ref, sec))
        one, two = a * b, a * roll(b)
        same = one if same is None else same + one
        cross = two if cross is None else cross + two
    low = low_half(same.shape)
    return jnp.where(low, same + roll(same), cross - roll(cross)) * scale


def tpu_roll(values):
    return pltpu.roll(values, LANES // 2, 1)


def ring_order(size):
    order = [size // 2]
    for step in range(size // 2 - 1, 0, -1):
        order += [step, size - step]
    return order


def kernel(
    chips, inner,
    x_ref, start_ref, stop_ref,
    first, ahead, back, last, ahead_turn, back_turn,
    out_ref,
    image, packed, own, far_a, far_b, spec, sends, gather, mixing,
    load_sem, send_sem, own_sem, pass_sem, far_sem, back_send, back_recv,
):
    devices = chips * CORES
    me = lax.axis_index("line")
    chip = me // CORES
    partner = chip * CORES + (CORES - 1 - me % CORES)
    date = lax.axis_index("date")
    dates = lax.axis_size("date")
    before = lax.rem(date + dates - 1, dates)
    after = lax.rem(date + 1, dates)
    load = pltpu.make_async_copy(x_ref.at[0], image, load_sem)
    load.start()

    barrier = pltpu.get_barrier_semaphore()

    def greet(i, _):
        pl.semaphore_signal(
            barrier, 1, device_id={"line": lax.rem(me + i, devices)}, device_id_type=MESH
        )
        return 0

    lax.fori_loop(1, devices, greet, 0)
    for row in (before, after):
        pl.semaphore_signal(barrier, 1, device_id={"date": row}, device_id_type=MESH)

    for i, piece in enumerate(first_table(first, devices)):
        mixing[i] = piece
    load.wait()

    def pack(t, _):
        rows = pl.ds(pl.multiple_of(t * 2 * GROUP, 2 * GROUP), 2 * GROUP)
        for k in range(2):
            lanes = slice(k * LANES, (k + 1) * LANES)
            real, imag = image[0, rows, lanes], image[1, rows, lanes]
            packed[t, k] = jnp.concatenate([real[:GROUP], imag[:GROUP]], 0)
            packed[t, 3 + k] = jnp.concatenate([real[GROUP:], imag[GROUP:]], 0)
        lanes = slice(2 * LANES, inner)
        real, imag = image[0, rows, lanes], image[1, rows, lanes]
        packed[t, 2] = jnp.concatenate(
            [
                jnp.concatenate([real[:GROUP], imag[:GROUP]], 0),
                jnp.concatenate([real[GROUP:], imag[GROUP:]], 0),
            ],
            1,
        )
        return 0

    lax.fori_loop(0, devices, pack, 0)
    pl.semaphore_wait(barrier, devices + 1)

    tiles = (pl.ds(0, 3), pl.ds(3, 2))
    order = ring_order(chips)

    def send(t, c):
        pltpu.make_async_remote_copy(
            packed.at[t, tiles[c]], own.at[me, tiles[c]], send_sem.at[c], own_sem.at[c, chip],
            device_id={"line": t}, device_id_type=MESH,
        ).start()

    for c in range(2):
        for o in order:
            t = lax.rem(chip + o, chips)
            for core in range(CORES):
                send(t * CORES + core, c)
        send(partner, c)
    own[me] = packed[me]

    passed = (pl.ds(0, 3), pl.ds(2, 3))
    fars = (far_a, far_b)
    rows_to = (before, after)

    def pass_on(s, c):
        pltpu.make_async_remote_copy(
            own.at[s, passed[c]], fars[c].at[s], pass_sem.at[c], far_sem.at[c],
            device_id={"date": rows_to[c]}, device_id_type=MESH,
        ).start()

    def take(c):
        one = own.at[pl.ds(0, 1), tiles[c]]
        pltpu.make_async_copy(one, one, own_sem.at[c, chip]).wait()
        for s in (me, partner):
            pass_on(s, c)
        for o in order:
            s = lax.rem(chip + chips - o, chips)
            both = own.at[pl.ds(0, CORES), tiles[c]]
            pltpu.make_async_copy(both, both, own_sem.at[c, s]).wait()
            for core in range(CORES):
                pass_on(s * CORES + core, c)

    rows = devices * GROUP
    scale = 1.0 / (LOOKS * float(devices * inner) ** 2)

    def tile(ref, k):
        return ref[:, k].reshape(2 * rows, LANES)

    def work(c):
        pair = (date, before)[c]
        start, stop = start_ref[pair], stop_ref[pair]
        turn = start_turn(ahead_turn, start, devices, inner)
        mine = [tile(own, k) for k in ((0, 1, 2), (3, 4, 2))[c]]
        theirs = [tile(fars[c], k) for k in ((0, 1, 2), (1, 2, 0))[c]]
        both = [mine, theirs] if c == 0 else [theirs, mine]
        lines = jnp.concatenate([lines_of(mixing, v, turn, c == 1, tpu_roll) for v in both], 0)
        spec[...] = right(lines, ahead)
        mask = keep_mask(start, stop, devices, rows)
        signals = []
        for i in range(2):
            part = spec[i * rows : (i + 1) * rows]
            signals.append(
                signal_of(back_lines(part, mask, back, back_turn, tpu_roll), last, tpu_roll)
            )
        result = looked(*signals, scale, tpu_roll)
        sends[c] = result.reshape(devices, GROUP, LANES)

    def give(c):
        row = (date, before)[c]
        skip = (1, 0)[c]

        def one(i, _):
            t = lax.rem(i + (me if skip else 0), devices)
            pltpu.make_async_remote_copy(
                sends.at[c, t], gather.at[c, me], back_send.at[c], back_recv.at[c],
                device_id={"line": t, "date": row}, device_id_type=MESH,
            ).start()
            return 0

        lax.fori_loop(skip, devices, one, 0)
        if skip:
            gather[c, me] = sends[c, me]

    def far_done(c):
        pltpu.make_async_copy(fars[c], fars[c], far_sem.at[c]).wait()

    take(0)
    far_done(0)
    work(0)
    give(0)
    take(1)
    far_done(1)
    work(1)
    give(1)

    for c in range(2):
        sent = own.at[pl.ds(0, devices - 1), tiles[c]]
        pltpu.make_async_copy(sent, sent, send_sem.at[c]).wait()
        pltpu.make_async_copy(fars[c], fars[c], pass_sem.at[c]).wait()
        whole = gather.at[c, pl.ds(0, devices - (1, 0)[c])]
        for sem in (back_send, back_recv):
            pltpu.make_async_copy(whole, whole, sem.at[c]).wait()

    half = LANES // 2
    joined = jnp.concatenate([gather[0], gather[1]], 1).reshape(2 * rows, LANES)
    out_ref[0, 0] = joined[:, :half]
    out_ref[0, 1] = joined[:, half:]


def shards(slc, band_start, band_stop):
    devices = lax.axis_size("line")
    chips = devices // CORES
    _, parts, columns, inner = slc.shape
    rows = devices * GROUP
    half = LANES // 2
    assert columns == devices * 2 * GROUP and inner == 2 * LANES + half
    constants = tables(devices, inner)
    hbm = pl.BlockSpec(memory_space=pltpu.HBM)
    vmem = pl.BlockSpec(memory_space=pltpu.VMEM)
    smem = pl.BlockSpec(memory_space=pltpu.SMEM)
    dma = pltpu.SemaphoreType.DMA
    f32 = jnp.float32
    return pl.pallas_call(
        functools.partial(kernel, chips, inner),
        out_shape=jax.ShapeDtypeStruct((1, parts, columns, inner // LOOKS), f32),
        in_specs=[hbm, smem, smem] + [vmem] * len(constants),
        out_specs=vmem,
        scratch_shapes=[
            pltpu.VMEM((parts, columns, inner), f32),
            pltpu.VMEM((devices, 5, 2 * GROUP, LANES), f32),
            pltpu.VMEM((devices, 5, 2 * GROUP, LANES), f32),
            pltpu.VMEM((devices, 3, 2 * GROUP, LANES), f32),
            pltpu.VMEM((devices, 3, 2 * GROUP, LANES), f32),
            pltpu.VMEM((2 * rows, 4 * LANES), f32),
            pltpu.VMEM((2, devices, GROUP, LANES), f32),
            pltpu.VMEM((2, devices, GROUP, LANES), f32),
            pltpu.VMEM((2, 2 * rows, 2 * rows), jnp.bfloat16),
            dma,
            dma((2,)),
            dma((2, chips)),
            dma((2,)),
            dma((2,)),
            dma((2,)),
            dma((2,)),
        ],
        compiler_params=pltpu.CompilerParams(collective_id=0, has_side_effects=True),
    )(slc, band_start, band_stop, *(jnp.asarray(c) for c in constants))


def solution(mesh):
    return jax.shard_map(
        shards,
        mesh=mesh,
        in_specs=(P("date", None, "stack", "line"), P(), P()),
        out_specs=P("date", None, "stack", "line"),
        check_vma=False,
    )
```

profile of v0, /device:TPU:65, one launch (start us, length us, event | category | flops | bytes accessed | tf_op | source)
XLA Modules:
  0.0 103.6 jit_solution(14396712363983274297)
XLA Ops:
  0.0 2.2 %copy.10.x_ref = f32[1,2,256,320]{3,2,1,0:T(8,128)} copy(f32[1,2,256,320]{2,3,1,0:T(8,128)} %param.9) | data formatting | bytes 1310720 | tf_op args[0]
  2.2 99.6 %shard_map.91 = f32[1,2,256,64]{3,2,1,0:T(8,128)} custom-call(f32[1,2,256,320]{3,2,1,0:T(8,128)} %copy.10.x_ref, s32[8]{0:T(128)} %start_ref.1, s32[8]{0:T(128)} %stop_ref.1, bf16[2,64,256]{2,1,0:T(8,128)(2,1)} %constant.12.clone.first, bf16[2,640,512]{2,1,0:T(8,128)(2,1)} %constant.13.clone.ahead, bf16[2,512,640]{2,1,0:T(8,128)(2,1)} %constant.14.clone.back, ...), custom_call_target="tpu_custom_call" | custom-call | tf_op jit(solution)/shard_map/pallas_call | solution.py:368
  101.8 1.7 %copy.11 = f32[1,2,256,64]{2,3,1,0:T(8,128)} copy(f32[1,2,256,64]{3,2,1,0:T(8,128)} %shard_map.91) | data formatting | bytes 262144 | tf_op jit(solution)/shard_map/pallas_call | solution.py:368
where the time goes:
time: 105 us; the launch traced here: 104 us
  Pallas kernels  99.6 us (95%)
  local copies, waits for them, and re-layouts  3.95 us (4%)
    pallas_call x1, Pallas kernels, shards(): pl.pallas_call(functools.partial(kernel, chips, inner), out_shape=jax.Sha...  99.6 us
    unnamed x1, local copies, waits for them, and re-layouts  2.23 us

commit v1 on v0

--- a/solution.py
+++ b/solution.py
@@ -12,6 +12,7 @@
 LOOKS = 5
 CORES = 2
 GROUP = 4
+EARLY = 5
 LANES = 128
 MESH = pl.DeviceIdType.MESH
 
@@ -139,10 +140,11 @@
     main = 2 * LANES
     tail_real, tail_imag = turned_real[:, main:], turned_imag[:, main:]
     low = low_half(tail_real.shape)
-    if second:
-        tail = jnp.where(low, roll(tail_real), tail_imag)
-    else:
-        tail = jnp.where(low, tail_real, roll(tail_imag))
+    tail = jnp.where(
+        second,
+        jnp.where(low, roll(tail_real), tail_imag),
+        jnp.where(low, tail_real, roll(tail_imag)),
+    )
     return jnp.concatenate([turned_real[:, :main], turned_imag[:, :main], tail], 1)
 
 
@@ -190,13 +192,39 @@
     return order
 
 
+def sublanes_turned(values):
+    return pltpu.roll(values, GROUP, 1)
+
+
+def pack(image, packed, inner):
+    columns = image.shape[2]
+    for h in range(columns // LANES):
+        lanes = slice(h * LANES, (h + 1) * LANES)
+        count = LANES // (2 * GROUP)
+        to = slice(h * count, (h + 1) * count)
+        shape = (count, 2 * GROUP, LANES)
+        upper = lax.broadcasted_iota(jnp.int32, shape, 1) < GROUP
+        for k in range(2):
+            lines = slice(k * LANES, (k + 1) * LANES)
+            real, imag = (image[i, lines, lanes].T.reshape(shape) for i in range(2))
+            packed[to, k] = jnp.where(upper, real, sublanes_turned(imag))
+            packed[to, 3 + k] = jnp.where(upper, sublanes_turned(real), imag)
+        tail = jnp.concatenate([image[i, 2 * LANES : inner, lanes] for i in range(2)], 0)
+        tail = tail.T
+        other = pltpu.roll(tail, LANES // 2, 1).reshape(shape)
+        tail = tail.reshape(shape)
+        low = lax.broadcasted_iota(jnp.int32, shape, 2) < LANES // 2
+        packed[to, 2] = jnp.where(upper == low, tail, sublanes_turned(other))
+
+
 def kernel(
-    chips, inner,
-    x_ref, start_ref, stop_ref,
-    first, ahead, back, last, ahead_turn, back_turn,
+    chips, early, inner,
+    x_ref, start_hbm, stop_hbm,
+    first_hbm, ahead_hbm, back_hbm, last_hbm, ahead_turn_hbm, back_turn_hbm,
     out_ref,
-    image, packed, own, far_a, far_b, spec, sends, gather, mixing,
-    load_sem, send_sem, own_sem, pass_sem, far_sem, back_send, back_recv,
+    image, packed, own, spec, sends, gather, mixing,
+    start_ref, stop_ref, first, ahead, back, last, ahead_turn, back_turn,
+    load_sem, table_sem, ready, known, prior, send_sem, own_sem, pass_sem, far_sem, back_send, back_recv,
 ):
     devices = chips * CORES
     me = lax.axis_index("line")
@@ -209,42 +237,54 @@
     load = pltpu.make_async_copy(x_ref.at[0], image, load_sem)
     load.start()
 
+    hubs = early - 1
+    hub = (me >= 1) & (me < early)
     barrier = pltpu.get_barrier_semaphore()
 
-    def greet(i, _):
-        pl.semaphore_signal(
-            barrier, 1, device_id={"line": lax.rem(me + i, devices)}, device_id_type=MESH
-        )
-        return 0
-
-    lax.fori_loop(1, devices, greet, 0)
+    def signal(sem, line):
+        pl.semaphore_signal(sem, 1, device_id={"line": line}, device_id_type=MESH)
+
+    def loop(low, high, body):
+        def step(i, _):
+            body(i)
+            return 0
+
+        lax.fori_loop(low, high, step, 0)
+
+    def others(low, high, body):
+        loop(low, high, lambda i: pl.when(i != me)(lambda: body(i)))
+
+    @pl.when(hub)
+    def _():
+        others(0, devices, lambda t: signal(barrier, t))
+
     for row in (before, after):
         pl.semaphore_signal(barrier, 1, device_id={"date": row}, device_id_type=MESH)
 
-    for i, piece in enumerate(first_table(first, devices)):
-        mixing[i] = piece
+    moves = [
+        pltpu.make_async_copy(source, to, table_sem.at[i])
+        for i, (source, to) in enumerate(
+            (
+                (first_hbm, first), (start_hbm, start_ref), (stop_hbm, stop_ref),
+                (ahead_turn_hbm, ahead_turn), (ahead_hbm, ahead), (back_hbm, back),
+                (back_turn_hbm, back_turn), (last_hbm, last),
+            )
+        )
+    ]
+
+    @pl.when(jnp.logical_not(hub))
+    def _():
+        pl.semaphore_wait(barrier, hubs + 2)
+        loop(1, early, lambda t: signal(ready.at[chip], t))
+
     load.wait()
-
-    def pack(t, _):
-        rows = pl.ds(pl.multiple_of(t * 2 * GROUP, 2 * GROUP), 2 * GROUP)
-        for k in range(2):
-            lanes = slice(k * LANES, (k + 1) * LANES)
-            real, imag = image[0, rows, lanes], image[1, rows, lanes]
-            packed[t, k] = jnp.concatenate([real[:GROUP], imag[:GROUP]], 0)
-            packed[t, 3 + k] = jnp.concatenate([real[GROUP:], imag[GROUP:]], 0)
-        lanes = slice(2 * LANES, inner)
-        real, imag = image[0, rows, lanes], image[1, rows, lanes]
-        packed[t, 2] = jnp.concatenate(
-            [
-                jnp.concatenate([real[:GROUP], imag[:GROUP]], 0),
-                jnp.concatenate([real[GROUP:], imag[GROUP:]], 0),
-            ],
-            1,
-        )
-        return 0
-
-    lax.fori_loop(0, devices, pack, 0)
-    pl.semaphore_wait(barrier, devices + 1)
+    for move in moves:
+        move.start()
+    pack(image, packed, inner)
+
+    @pl.when(hub)
+    def _():
+        pl.semaphore_wait(barrier, hubs + 1)
 
     tiles = (pl.ds(0, 3), pl.ds(3, 2))
     order = ring_order(chips)
@@ -255,101 +295,172 @@
             device_id={"line": t}, device_id_type=MESH,
         ).start()
 
+    def ring(body):
+        for o in order:
+            t = lax.rem(chip + o, chips) * CORES
+            for core in range(CORES):
+                body(t + core)
+        body(partner)
+
     for c in range(2):
-        for o in order:
-            t = lax.rem(chip + o, chips)
-            for core in range(CORES):
-                send(t * CORES + core, c)
-        send(partner, c)
-    own[me] = packed[me]
+        ring(lambda t: pl.when((t >= 1) & (t < early))(lambda: send(t, c)))
+
+    def send_both(t):
+        for c in range(2):
+            send(t, c)
+
+    def send_chip(k):
+        for core in range(CORES):
+            send_both(k * CORES + core)
+
+    first_chip = early // CORES
+
+    @pl.when(hub)
+    def _():
+        teller = me == 1
+
+        def meet(k):
+            pl.semaphore_wait(ready.at[k], CORES)
+
+            @pl.when(teller)
+            def _():
+                for core in range(CORES):
+                    signal(prior, k * CORES + core)
+                loop(early, k * CORES, lambda t: signal(known.at[k], t))
+                pl.when(k == chips - 1)(lambda: signal(known.at[k], 0))
+
+            send_chip(k)
+
+        loop(first_chip, chips - 1, meet)
+        pl.semaphore_wait(ready.at[0], 1)
+
+        @pl.when(teller)
+        def _():
+            signal(prior, 0)
+            loop(early, devices - CORES, lambda t: signal(known.at[0], t))
+
+        send_both(0)
+        meet(chips - 1)
+
+    @pl.when(jnp.logical_not(hub))
+    def _():
+        zero = me == 0
+        end = chip == chips - 1
+        pl.semaphore_wait(prior, 1)
+        pl.when(jnp.logical_not(zero))(lambda: send_both(partner))
+        pl.when(end)(lambda: send_both(0))
+        loop(first_chip, jnp.where(zero, chips - 1, chip), send_chip)
+
+        def meet(k):
+            pl.semaphore_wait(known.at[k], 1)
+            send_chip(k)
+
+        loop(jnp.where(zero, chips, chip + 1), chips - 1, meet)
+
+        @pl.when(jnp.logical_not(zero | end))
+        def _():
+            pl.semaphore_wait(known.at[0], 1)
+            send_both(0)
+
+        pl.when(jnp.logical_not(end))(lambda: meet(chips - 1))
+
+    own[me, 0:5] = packed[me]
+    for move in moves:
+        move.wait()
+    for i, piece in enumerate(first_table(first, devices)):
+        mixing[i] = piece
 
     passed = (pl.ds(0, 3), pl.ds(2, 3))
-    fars = (far_a, far_b)
+    passed_to = (pl.ds(5, 3), pl.ds(8, 3))
     rows_to = (before, after)
 
     def pass_on(s, c):
         pltpu.make_async_remote_copy(
-            own.at[s, passed[c]], fars[c].at[s], pass_sem.at[c], far_sem.at[c],
+            own.at[s, passed[c]], own.at[s, passed_to[c]], pass_sem.at[c], far_sem.at[c],
             device_id={"date": rows_to[c]}, device_id_type=MESH,
         ).start()
 
-    def take(c):
-        one = own.at[pl.ds(0, 1), tiles[c]]
-        pltpu.make_async_copy(one, one, own_sem.at[c, chip]).wait()
-        for s in (me, partner):
-            pass_on(s, c)
-        for o in order:
-            s = lax.rem(chip + chips - o, chips)
-            both = own.at[pl.ds(0, CORES), tiles[c]]
-            pltpu.make_async_copy(both, both, own_sem.at[c, s]).wait()
+    def take(s, count):
+        for c in range(2):
+            new = own.at[pl.ds(0, count), tiles[c]]
+            pltpu.make_async_copy(new, new, own_sem.at[c, s]).wait()
             for core in range(CORES):
                 pass_on(s * CORES + core, c)
 
     rows = devices * GROUP
     scale = 1.0 / (LOOKS * float(devices * inner) ** 2)
 
-    def tile(ref, k):
-        return ref[:, k].reshape(2 * rows, LANES)
-
-    def work(c):
-        pair = (date, before)[c]
+    def tile(k):
+        return own[:, k].reshape(2 * rows, LANES)
+
+    def image_signal(c, far):
+        pair = jnp.where(c == 0, date, before)
         start, stop = start_ref[pair], stop_ref[pair]
         turn = start_turn(ahead_turn, start, devices, inner)
-        mine = [tile(own, k) for k in ((0, 1, 2), (3, 4, 2))[c]]
-        theirs = [tile(fars[c], k) for k in ((0, 1, 2), (1, 2, 0))[c]]
-        both = [mine, theirs] if c == 0 else [theirs, mine]
-        lines = jnp.concatenate([lines_of(mixing, v, turn, c == 1, tpu_roll) for v in both], 0)
-        spec[...] = right(lines, ahead)
+        main = 3 * c + far * (5 + c)
+        tail = 2 + far * (5 + c)
+        block = [tile(main), tile(main + 1), tile(tail)]
+        lines = lines_of(mixing, block, turn, c == 1, tpu_roll)
         mask = keep_mask(start, stop, devices, rows)
-        signals = []
-        for i in range(2):
-            part = spec[i * rows : (i + 1) * rows]
-            signals.append(
-                signal_of(back_lines(part, mask, back, back_turn, tpu_roll), last, tpu_roll)
-            )
-        result = looked(*signals, scale, tpu_roll)
-        sends[c] = result.reshape(devices, GROUP, LANES)
+        kept = back_lines(right(lines, ahead), mask, back, back_turn, tpu_roll)
+        return signal_of(kept, last, tpu_roll)
 
     def give(c):
-        row = (date, before)[c]
-        skip = (1, 0)[c]
-
-        def one(i, _):
-            t = lax.rem(i + (me if skip else 0), devices)
+        row = jnp.where(c == 0, date, before)
+
+        def one(t):
             pltpu.make_async_remote_copy(
                 sends.at[c, t], gather.at[c, me], back_send.at[c], back_recv.at[c],
                 device_id={"line": t, "date": row}, device_id_type=MESH,
             ).start()
-            return 0
-
-        lax.fori_loop(skip, devices, one, 0)
-        if skip:
+
+        loop(0, devices, lambda t: pl.when((c == 1) | (t != me))(lambda: one(t)))
+
+        @pl.when(c == 0)
+        def _():
             gather[c, me] = sends[c, me]
 
-    def far_done(c):
-        pltpu.make_async_copy(fars[c], fars[c], far_sem.at[c]).wait()
-
-    take(0)
-    far_done(0)
-    work(0)
-    give(0)
-    take(1)
-    far_done(1)
-    work(1)
-    give(1)
+    take(chip, 1)
+    for o in order[::-1]:
+        take(lax.rem(chip + chips - o, chips), CORES)
+
+    def image_of(i):
+        c, far = lax.rem(i, 2), i // 2
+
+        @pl.when(far == 1)
+        def _():
+            new = own.at[:, pl.ds(5, 3)]
+            pltpu.make_async_copy(new, new, far_sem.at[c]).wait()
+
+        spec[i] = image_signal(c, far)
+
+        @pl.when(far == 1)
+        def _():
+            ref, sec = spec[i - 2 + 2 * c], spec[i - 2 * c]
+            sends[c] = looked(ref, sec, scale, tpu_roll).reshape(devices, GROUP, LANES)
+            give(c)
+
+    loop(0, 4, image_of)
+
+    for c in range(2):
+        whole = gather.at[c, pl.ds(0, devices - (1, 0)[c])]
+        pltpu.make_async_copy(whole, whole, back_recv.at[c]).wait()
+
+    half = LANES // 2
+    joined = jnp.concatenate([gather[0], gather[1]], 1).reshape(2 * rows, LANES)
+    for h in range(2 * rows // LANES):
+        lanes = slice(h * LANES, (h + 1) * LANES)
+        both = joined[lanes].T
+        out_ref[0, 0, :, lanes] = both[:half]
+        out_ref[0, 1, :, lanes] = both[half:]
 
     for c in range(2):
         sent = own.at[pl.ds(0, devices - 1), tiles[c]]
         pltpu.make_async_copy(sent, sent, send_sem.at[c]).wait()
-        pltpu.make_async_copy(fars[c], fars[c], pass_sem.at[c]).wait()
+        new = own.at[:, pl.ds(5, 3)]
+        pltpu.make_async_copy(new, new, pass_sem.at[c]).wait()
         whole = gather.at[c, pl.ds(0, devices - (1, 0)[c])]
-        for sem in (back_send, back_recv):
-            pltpu.make_async_copy(whole, whole, sem.at[c]).wait()
-
-    half = LANES // 2
-    joined = jnp.concatenate([gather[0], gather[1]], 1).reshape(2 * rows, LANES)
-    out_ref[0, 0] = joined[:, :half]
-    out_ref[0, 1] = joined[:, half:]
+        pltpu.make_async_copy(whole, whole, back_send.at[c]).wait()
 
 
 def shards(slc, band_start, band_stop):
@@ -359,28 +470,32 @@
     rows = devices * GROUP
     half = LANES // 2
     assert columns == devices * 2 * GROUP and inner == 2 * LANES + half
-    constants = tables(devices, inner)
+    constants = [jnp.asarray(c) for c in tables(devices, inner)]
     hbm = pl.BlockSpec(memory_space=pltpu.HBM)
-    vmem = pl.BlockSpec(memory_space=pltpu.VMEM)
-    smem = pl.BlockSpec(memory_space=pltpu.SMEM)
     dma = pltpu.SemaphoreType.DMA
+    count = pltpu.SemaphoreType.REGULAR
     f32 = jnp.float32
-    return pl.pallas_call(
-        functools.partial(kernel, chips, inner),
-        out_shape=jax.ShapeDtypeStruct((1, parts, columns, inner // LOOKS), f32),
-        in_specs=[hbm, smem, smem] + [vmem] * len(constants),
-        out_specs=vmem,
+    result = pl.pallas_call(
+        functools.partial(kernel, chips, EARLY * devices // 8, inner),
+        out_shape=jax.ShapeDtypeStruct((1, parts, inner // LOOKS, columns), f32),
+        in_specs=[hbm] * (3 + len(constants)),
+        out_specs=pl.BlockSpec(memory_space=pltpu.VMEM),
         scratch_shapes=[
-            pltpu.VMEM((parts, columns, inner), f32),
+            pltpu.VMEM((parts, inner, columns), f32),
             pltpu.VMEM((devices, 5, 2 * GROUP, LANES), f32),
-            pltpu.VMEM((devices, 5, 2 * GROUP, LANES), f32),
-            pltpu.VMEM((devices, 3, 2 * GROUP, LANES), f32),
-            pltpu.VMEM((devices, 3, 2 * GROUP, LANES), f32),
-            pltpu.VMEM((2 * rows, 4 * LANES), f32),
+            pltpu.VMEM((devices, 11, 2 * GROUP, LANES), f32),
+            pltpu.VMEM((4, rows, 2 * inner), f32),
             pltpu.VMEM((2, devices, GROUP, LANES), f32),
             pltpu.VMEM((2, devices, GROUP, LANES), f32),
             pltpu.VMEM((2, 2 * rows, 2 * rows), jnp.bfloat16),
+            pltpu.SMEM(band_start.shape, jnp.int32),
+            pltpu.SMEM(band_stop.shape, jnp.int32),
+            *(pltpu.VMEM(c.shape, c.dtype) for c in constants),
             dma,
+            dma((8,)),
+            count((chips,)),
+            count((chips,)),
+            count,
             dma((2,)),
             dma((2, chips)),
             dma((2,)),
@@ -389,7 +504,8 @@
             dma((2,)),
         ],
         compiler_params=pltpu.CompilerParams(collective_id=0, has_side_effects=True),
-    )(slc, band_start, band_stop, *(jnp.asarray(c) for c in constants))
+    )(jnp.swapaxes(slc, 2, 3), band_start, band_stop, *constants)
+    return jnp.swapaxes(result, 2, 3)
 
 
 def solution(mesh):

time: 105 us -> 92.8 us (0.88); the launches traced: 104 us -> 92.6 us
  Pallas kernels: 99.6 us -> 91.1 us
  local copies, waits for them, and re-layouts: 3.95 us -> 1.57 us
    pallas_call x1, Pallas kernels: 99.6 us -> 91.1 us  [shards(): pl.pallas_call(functools.partial(kernel, chips, EARLY * devices // 8, inn...]
    pallas_call x1 -> x0, local copies, waits for them, and re-layouts: 1.72 us -> none  [shards(): pl.pallas_call(functools.partial(kernel, chips, inner), out_shape=jax.Sha...]
where the time goes in v1:
time: 92.8 us; the launch traced here: 92.6 us
  Pallas kernels  91.1 us (98%)
  local copies, waits for them, and re-layouts  1.57 us (2%)
    pallas_call x1, Pallas kernels, shards(): pl.pallas_call(functools.partial(kernel, chips, EARLY * devices // 8, inn...  91.1 us

profile of v1, /device:TPU:65, one launch (start us, length us, event | category | flops | bytes accessed | tf_op | source)
XLA Modules:
  0.0 92.6 jit_solution(14777221035070980807)
XLA Ops:
  0.0 91.1 %shard_map.91 = f32[1,2,64,256]{3,2,1,0:T(8,128)} custom-call(f32[1,2,320,256]{3,2,1,0:T(8,128)} %bitcast.2, s32[8]{0:T(128)} %start_hbm.1, s32[8]{0:T(128)} %stop_hbm.1, bf16[2,64,256]{2,1,0:T(8,128)(2,1)} %constant.12.clone.first_hbm, bf16[2,640,512]{2,1,0:T(8,128)(2,1)} %constant.13.clone.ahead_hbm, bf16[2,512,640]{2,1,0:T(8,128)(2,1)} %constant.14.clone.back_hbm, ...), custom_call_target="tpu_custom_call" | custom-call | tf_op jit(solution)/shard_map/pallas_call | solution.py:478
  91.1 1.6 %copy.11 = f32[1,2,256,64]{2,3,1,0:T(8,128)} copy(f32[1,2,256,64]{2,3,1,0:T(8,128)} %bitcast.3) | data formatting | bytes 262144

commit v2 on v1

--- a/solution.py
+++ b/solution.py
@@ -405,7 +405,7 @@
         kept = back_lines(right(lines, ahead), mask, back, back_turn, tpu_roll)
         return signal_of(kept, last, tpu_roll)
 
-    def give(c):
+    def give(c, low, high):
         row = jnp.where(c == 0, date, before)
 
         def one(t):
@@ -414,15 +414,12 @@
                 device_id={"line": t, "date": row}, device_id_type=MESH,
             ).start()
 
-        loop(0, devices, lambda t: pl.when((c == 1) | (t != me))(lambda: one(t)))
-
-        @pl.when(c == 0)
-        def _():
-            gather[c, me] = sends[c, me]
+        loop(low, high, lambda t: pl.when((c == 1) | (t != me))(lambda: one(t)))
 
     take(chip, 1)
-    for o in order[::-1]:
-        take(lax.rem(chip + chips - o, chips), CORES)
+    loop(1, chips - 1, lambda s: pl.when(s != chip)(lambda: take(s, CORES)))
+    pl.when(chip != 0)(lambda: take(0, CORES))
+    pl.when(chip != chips - 1)(lambda: take(chips - 1, CORES))
 
     def image_of(i):
         c, far = lax.rem(i, 2), i // 2
@@ -438,9 +435,12 @@
         def _():
             ref, sec = spec[i - 2 + 2 * c], spec[i - 2 * c]
             sends[c] = looked(ref, sec, scale, tpu_roll).reshape(devices, GROUP, LANES)
-            give(c)
+            give(c, 0, devices // 4)
 
     loop(0, 4, image_of)
+    for c in range(2):
+        give(c, devices // 4, devices)
+    gather[0, me] = sends[0, me]
 
     for c in range(2):
         whole = gather.at[c, pl.ds(0, devices - (1, 0)[c])]
@@ -477,7 +477,7 @@
     f32 = jnp.float32
     result = pl.pallas_call(
         functools.partial(kernel, chips, EARLY * devices // 8, inner),
-        out_shape=jax.ShapeDtypeStruct((1, parts, inner // LOOKS, columns), f32),
+        out_shape=pltpu.VMEM((1, parts, inner // LOOKS, columns), f32),
         in_specs=[hbm] * (3 + len(constants)),
         out_specs=pl.BlockSpec(memory_space=pltpu.VMEM),
         scratch_shapes=[

time: 92.8 us -> 90.3 us (0.973)
  Pallas kernels: 91.1 us -> 89.2 us
    pallas_call x1, Pallas kernels: 91.1 us -> 89.2 us  [shards(): pl.pallas_call(functools.partial(kernel, chips, EARLY * devices // 8, inn...]
where the time goes in v2:
time: 90.3 us; the launch traced here: 89.8 us
  Pallas kernels  89.2 us (99%)
    pallas_call x1, Pallas kernels, shards(): pl.pallas_call(functools.partial(kernel, chips, EARLY * devices // 8, inn...  89.2 us

profile of v2, /device:TPU:65, one launch (start us, length us, event | category | flops | bytes accessed | tf_op | source)
XLA Modules:
  0.0 89.8 jit_solution(15471615240518623421)
XLA Ops:
  0.0 89.2 %shard_map.91 = f32[1,2,64,256]{3,2,1,0:T(8,128)S(1)} custom-call(f32[1,2,320,256]{3,2,1,0:T(8,128)} %bitcast.3, s32[8]{0:T(128)} %start_hbm.1, s32[8]{0:T(128)} %stop_hbm.1, bf16[2,64,256]{2,1,0:T(8,128)(2,1)} %constant.12.clone.first_hbm, bf16[2,640,512]{2,1,0:T(8,128)(2,1)} %constant.13.clone.ahead_hbm, bf16[2,512,640]{2,1,0:T(8,128)(2,1)} %constant.14.clone.back_hbm, ...), custom_call_target="tpu_custom_call" | custom-call | tf_op jit(solution)/shard_map/pallas_call | solution.py:478
  89.2 0.7 copy.11

commit v3 on v2

--- a/solution.py
+++ b/solution.py
@@ -12,7 +12,7 @@
 LOOKS = 5
 CORES = 2
 GROUP = 4
-EARLY = 5
+EARLY = 4
 LANES = 128
 MESH = pl.DeviceIdType.MESH
 
@@ -286,12 +286,12 @@
     def _():
         pl.semaphore_wait(barrier, hubs + 1)
 
-    tiles = (pl.ds(0, 3), pl.ds(3, 2))
+    message = pl.ds(0, 5)
     order = ring_order(chips)
 
-    def send(t, c):
+    def send(t):
         pltpu.make_async_remote_copy(
-            packed.at[t, tiles[c]], own.at[me, tiles[c]], send_sem.at[c], own_sem.at[c, chip],
+            packed.at[t], own.at[me, message], send_sem, own_sem.at[chip],
             device_id={"line": t}, device_id_type=MESH,
         ).start()
 
@@ -302,16 +302,11 @@
                 body(t + core)
         body(partner)
 
-    for c in range(2):
-        ring(lambda t: pl.when((t >= 1) & (t < early))(lambda: send(t, c)))
-
-    def send_both(t):
-        for c in range(2):
-            send(t, c)
+    ring(lambda t: pl.when((t >= 1) & (t < early))(lambda: send(t)))
 
     def send_chip(k):
         for core in range(CORES):
-            send_both(k * CORES + core)
+            send(k * CORES + core)
 
     first_chip = early // CORES
 
@@ -339,7 +334,7 @@
             signal(prior, 0)
             loop(early, devices - CORES, lambda t: signal(known.at[0], t))
 
-        send_both(0)
+        send(0)
         meet(chips - 1)
 
     @pl.when(jnp.logical_not(hub))
@@ -347,8 +342,8 @@
         zero = me == 0
         end = chip == chips - 1
         pl.semaphore_wait(prior, 1)
-        pl.when(jnp.logical_not(zero))(lambda: send_both(partner))
-        pl.when(end)(lambda: send_both(0))
+        pl.when(jnp.logical_not(zero))(lambda: send(partner))
+        pl.when(end)(lambda: send(0))
         loop(first_chip, jnp.where(zero, chips - 1, chip), send_chip)
 
         def meet(k):
@@ -360,7 +355,7 @@
         @pl.when(jnp.logical_not(zero | end))
         def _():
             pl.semaphore_wait(known.at[0], 1)
-            send_both(0)
+            send(0)
 
         pl.when(jnp.logical_not(end))(lambda: meet(chips - 1))
 
@@ -375,17 +370,17 @@
     rows_to = (before, after)
 
     def pass_on(s, c):
+        lines = pl.ds(s * CORES, CORES)
         pltpu.make_async_remote_copy(
-            own.at[s, passed[c]], own.at[s, passed_to[c]], pass_sem.at[c], far_sem.at[c],
+            own.at[lines, passed[c]], own.at[lines, passed_to[c]], pass_sem.at[c], far_sem.at[c],
             device_id={"date": rows_to[c]}, device_id_type=MESH,
         ).start()
 
     def take(s, count):
+        new = own.at[pl.ds(0, count), message]
+        pltpu.make_async_copy(new, new, own_sem.at[s]).wait()
         for c in range(2):
-            new = own.at[pl.ds(0, count), tiles[c]]
-            pltpu.make_async_copy(new, new, own_sem.at[c, s]).wait()
-            for core in range(CORES):
-                pass_on(s * CORES + core, c)
+            pass_on(s, c)
 
     rows = devices * GROUP
     scale = 1.0 / (LOOKS * float(devices * inner) ** 2)
@@ -454,9 +449,9 @@
         out_ref[0, 0, :, lanes] = both[:half]
         out_ref[0, 1, :, lanes] = both[half:]
 
+    sent = own.at[pl.ds(0, devices - 1), message]
+    pltpu.make_async_copy(sent, sent, send_sem).wait()
     for c in range(2):
-        sent = own.at[pl.ds(0, devices - 1), tiles[c]]
-        pltpu.make_async_copy(sent, sent, send_sem.at[c]).wait()
         new = own.at[:, pl.ds(5, 3)]
         pltpu.make_async_copy(new, new, pass_sem.at[c]).wait()
         whole = gather.at[c, pl.ds(0, devices - (1, 0)[c])]
@@ -496,8 +491,8 @@
             count((chips,)),
             count((chips,)),
             count,
-            dma((2,)),
-            dma((2, chips)),
+            dma,
+            dma((chips,)),
             dma((2,)),
             dma((2,)),
             dma((2,)),

time: 90.3 us -> 89.5 us (level)
  Pallas kernels: 89.2 us -> 88.2 us
    pallas_call x1, Pallas kernels: 89.2 us -> 88.2 us  [shards(): pl.pallas_call(functools.partial(kernel, chips, EARLY * devices // 8, inn...]
where the time goes in v3:
time: 89.5 us; the launch traced here: 88.8 us
  Pallas kernels  88.2 us (99%)
    pallas_call x1, Pallas kernels, shards(): pl.pallas_call(functools.partial(kernel, chips, EARLY * devices // 8, inn...  88.2 us

profile of v3, /device:TPU:65, one launch (start us, length us, event | category | flops | bytes accessed | tf_op | source)
XLA Modules:
  0.0 88.8 jit_solution(698842752548705391)
XLA Ops:
  0.0 88.2 %shard_map.91 = f32[1,2,64,256]{3,2,1,0:T(8,128)S(1)} custom-call(f32[1,2,320,256]{3,2,1,0:T(8,128)} %bitcast.3, s32[8]{0:T(128)} %start_hbm.1, s32[8]{0:T(128)} %stop_hbm.1, bf16[2,64,256]{2,1,0:T(8,128)(2,1)} %constant.12.clone.first_hbm, bf16[2,640,512]{2,1,0:T(8,128)(2,1)} %constant.13.clone.ahead_hbm, bf16[2,512,640]{2,1,0:T(8,128)(2,1)} %constant.14.clone.back_hbm, ...), custom_call_target="tpu_custom_call" | custom-call | tf_op jit(solution)/shard_map/pallas_call | solution.py:473
  88.2 0.7 copy.11
